TPU v7x, 256 devices: a whole 4x4x8 slice. The times are simulated.
256 devices in a mesh: tm: 32 (over x_hi, z, core), freq: 8 (over x_lo, y).
Axes of the slice: x: 4 (x_hi: 2, x_lo: 2; x = x_hi * 2 + x_lo), y: 4, z: 8, core: 2. Of those that a mesh axis runs over, the one named last changes fastest.
Arguments:
- strengths: bfloat16 [2, 8, 256, 65536], P(None, 'freq', None, 'tm'), may hold values from -6 to 6
- sample_cell: int32 [65536], P('tm'), may hold values from 0 to 32767, as said below
- sample_frac: float32 [65536], P('tm'), may hold values from 0 to 1
Outputs:
- spectra: float32 [2, 8, 256, 8, 32, 128], P(None, None, 'tm', 'freq')
Inputs may be any that keep to these rules, and one draw needn't show every extreme that they name: `sample_cell`: the samples of the i-th aligned block of 2048 samples lie in cells i * 1024 to (i + 1) * 1024 - 1; in every block the first sample lies in the first of these cells and the second sample in the last.
All inputs are finite; a program needn't handle non-finite values.
Results may differ from a plain program's by a relative error of at most 0.0037.
Values may be sent and summed in bfloat16 or wider, within the bound.
A program may use at most 128 MiB of HBM per device.

v0:
```python
import math

import jax
import jax.numpy as jnp
from jax import lax
from jax.sharding import PartitionSpec as P

TAPS = 8
GRID_DEV = 1024
FFT_LO = 32
FFT_HI = 128
FFTLEN = 4096


sharpness = 0.3


def with_halo(cells, sides, width):
    for axis, dim in sides:
        count = lax.axis_size(axis)
        head = lax.slice_in_dim(cells, 0, width, axis=dim)
        tail = lax.slice_in_dim(cells, cells.shape[dim] - width, cells.shape[dim], axis=dim)
        cells = jnp.concatenate(
            [
                lax.ppermute(tail, axis, [(i, (i + 1) % count) for i in range(count)]),
                cells,
                lax.ppermute(head, axis, [((i + 1) % count, i) for i in range(count)]),
            ],
            axis=dim,
        )
    return cells


def tap_table(local_cell, fraction, columns):
    offset = columns[None, :] - local_cell[:, None] - 1
    inside = (offset >= 0) & (offset < TAPS)
    shifted = offset.astype(jnp.float32) - float(TAPS // 2 - 1) - fraction[:, None]
    values = jnp.exp(-sharpness * (shifted * shifted))
    return jnp.where(inside, values, 0.0).astype(jnp.bfloat16)


def spread(strength_rows, local_cell, fraction, columns):
    sample_count = strength_rows.shape[1]
    block_len = 512
    block_count = sample_count // block_len

    def accumulate(block_index, running_sum):
        block_start = block_index * block_len
        sample_block = lax.dynamic_slice_in_dim(strength_rows, block_start, block_len, 1)
        cell_block = lax.dynamic_slice_in_dim(local_cell, block_start, block_len, 0)
        frac_block = lax.dynamic_slice_in_dim(fraction, block_start, block_len, 0)
        weight_table = tap_table(cell_block, frac_block, columns)
        return running_sum + jnp.dot(sample_block, weight_table, preferred_element_type=jnp.float32)

    initial = jnp.zeros((strength_rows.shape[0], columns.shape[0]), jnp.float32)
    return lax.fori_loop(0, block_count, accumulate, initial)


def frames_transform(grid_bf16):
    groups_all = grid_bf16.shape[1]
    channels = grid_bf16.shape[2]
    frames = grid_bf16.shape[3] // FFTLEN
    signal = grid_bf16.astype(jnp.float32).reshape(2, groups_all, channels, frames, FFT_LO, FFT_HI)
    real_in = signal[0]
    imag_in = signal[1]
    low_index = jnp.arange(FFT_LO, dtype=jnp.int32)
    high_index = jnp.arange(FFT_HI, dtype=jnp.int32)
    low_angle = (
        2.0
        * math.pi
        / FFT_LO
        * (low_index[:, None] * low_index[None, :] % FFT_LO).astype(jnp.float32)
    )
    high_angle = (
        2.0
        * math.pi
        / FFT_HI
        * (high_index[:, None] * high_index[None, :] % FFT_HI).astype(jnp.float32)
    )
    twist_angle = (
        2.0 * math.pi / FFTLEN * (low_index[:, None] * high_index[None, :]).astype(jnp.float32)
    )
    low_cos = jnp.cos(low_angle)
    low_sin = jnp.sin(low_angle)
    high_cos = jnp.cos(high_angle)
    high_sin = jnp.sin(high_angle)
    twist_cos = jnp.cos(twist_angle)
    twist_sin = jnp.sin(twist_angle)
    level = lax.Precision.HIGH
    section_real = jnp.einsum("kn,...nm->...km", low_cos, real_in, precision=level) + jnp.einsum(
        "kn,...nm->...km", low_sin, imag_in, precision=level
    )
    section_imag = jnp.einsum("kn,...nm->...km", low_cos, imag_in, precision=level) - jnp.einsum(
        "kn,...nm->...km", low_sin, real_in, precision=level
    )
    turned_real = section_real * twist_cos + section_imag * twist_sin
    turned_imag = section_imag * twist_cos - section_real * twist_sin
    out_real = jnp.einsum("...an,nb->...ab", turned_real, high_cos, precision=level) + jnp.einsum(
        "...an,nb->...ab", turned_imag, high_sin, precision=level
    )
    out_imag = jnp.einsum("...an,nb->...ab", turned_imag, high_cos, precision=level) - jnp.einsum(
        "...an,nb->...ab", turned_real, high_sin, precision=level
    )
    normalizer = 1.0 / math.sqrt(FFTLEN)
    return jnp.stack([out_real, out_imag]) * normalizer


def shards(strengths, sample_cell, sample_frac):
    half_taps = TAPS // 2
    groups_here = strengths.shape[1]
    channels = strengths.shape[2]
    sample_count = strengths.shape[3]
    block_cells = GRID_DEV
    strength_rows = strengths.reshape(2 * groups_here * channels, sample_count)
    local_cell = sample_cell - lax.axis_index("tm") * block_cells
    extended = spread(
        strength_rows, local_cell, sample_frac, jnp.arange(block_cells + TAPS, dtype=jnp.int32)
    )
    padded = with_halo(extended, (("tm", 1),), half_taps)
    interior = extended[:, half_taps : half_taps + block_cells]
    summed = (
        interior.at[:, :half_taps]
        .add(padded[:, :half_taps])
        .at[:, block_cells - half_taps :]
        .add(padded[:, -half_taps:])
    )
    rounded = summed.astype(jnp.bfloat16).reshape(2, groups_here, channels, block_cells)
    arranged = lax.all_to_all(
        lax.all_to_all(rounded, "tm", split_axis=2, concat_axis=3, tiled=True),
        "freq",
        split_axis=3,
        concat_axis=1,
        tiled=True,
    )
    return frames_transform(arranged)


def solution(mesh):
    placed = (P(None, "freq", None, "tm"), P("tm"), P("tm"))
    return jax.shard_map(
        shards,
        mesh=mesh,
        in_specs=placed,
        out_specs=P(None, None, "tm", "freq", None, None),
        check_vma=False,
    )
```

profile of v0, /device:TPU:11, one launch (start us, length us, event | category | flops | bytes accessed | tf_op | source)
XLA Modules:
  0.0 194.4 jit_solution(15310372515523897435)
XLA Ops:
  0.0 0.7 broadcast_subtract_fusion
  0.7 15.8 %while.18 = (s32[]{:T(128)}, f32[512,1032]{0,1:T(8,128)S(1)}, bf16[512,2048]{1,0:T(8,128)(2,1)}, s32[2048]{0:T(1024)S(1)}, f32[2048]{0:T(1024)}, /*index=5*/s32[]{:T(128)}, s32[]{:T(128)}, s32[]{:T(128)}, s32[]{:T(128)}) while((s32[]{:T(128)}, f32[512,1032]{0,1:T(8,128)S(1)}, bf16[512,2048]{1,0:T(8,128)(2,1)}, s32[2048]{0:T(1024)S(1)}, ...), condition=%wide.region_1.2_spmd.clone, body=%wide.region_0.1_spmd.clone.sunk | while | flops 548462592 | bytes 4763809 | solution.py:56
  0.7 0.8 dynamic_slice.39
  1.5 0.1 dynamic_slice.40
  1.5 3.1 %convolution_add_fusion.4 = f32[512,1032]{0,1:T(8,128)S(1)} fusion(f32[512,1032]{0,1:T(8,128)S(1)} %get-tuple-element.262, f32[512]{0:T(512)S(1)} %dynamic_slice.39, s32[512]{0:T(512)S(1)} %dynamic_slice.40, pred[]{:T(512)S(6)} %compare.19, bf16[512,2048]{1,0:T(8,128)(2,1)} %get-tuple-element.272, s32[]{:T(128)S(6)} %select_n.101), kind=kOutput, calls=%fused_computation.1.clone.1 | convolution fusion | flops 548462592 | bytes 4755461 | tf_op jit(solution)/shard_map/while/body/eval_jaxpr/dot_general | solution.py:53
  4.7 0.8 dynamic_slice.39
  5.4 0.1 dynamic_slice.40
  5.5 3.1 %convolution_add_fusion.4 = f32[512,1032]{0,1:T(8,128)S(1)} fusion(f32[512,1032]{0,1:T(8,128)S(1)} %get-tuple-element.262, f32[512]{0:T(512)S(1)} %dynamic_slice.39, s32[512]{0:T(512)S(1)} %dynamic_slice.40, pred[]{:T(512)S(6)} %compare.19, bf16[512,2048]{1,0:T(8,128)(2,1)} %get-tuple-element.272, s32[]{:T(128)S(6)} %select_n.101), kind=kOutput, calls=%fused_computation.1.clone.1 | convolution fusion | flops 548462592 | bytes 4755461 | tf_op jit(solution)/shard_map/while/body/eval_jaxpr/dot_general | solution.py:53
  8.6 0.8 dynamic_slice.39
  9.4 0.1 dynamic_slice.40
  9.5 3.1 %convolution_add_fusion.4 = f32[512,1032]{0,1:T(8,128)S(1)} fusion(f32[512,1032]{0,1:T(8,128)S(1)} %get-tuple-element.262, f32[512]{0:T(512)S(1)} %dynamic_slice.39, s32[512]{0:T(512)S(1)} %dynamic_slice.40, pred[]{:T(512)S(6)} %compare.19, bf16[512,2048]{1,0:T(8,128)(2,1)} %get-tuple-element.272, s32[]{:T(128)S(6)} %select_n.101), kind=kOutput, calls=%fused_computation.1.clone.1 | convolution fusion | flops 548462592 | bytes 4755461 | tf_op jit(solution)/shard_map/while/body/eval_jaxpr/dot_general | solution.py:53
  12.6 0.8 dynamic_slice.39
  13.3 0.1 dynamic_slice.40
  13.4 3.1 %convolution_add_fusion.4 = f32[512,1032]{0,1:T(8,128)S(1)} fusion(f32[512,1032]{0,1:T(8,128)S(1)} %get-tuple-element.262, f32[512]{0:T(512)S(1)} %dynamic_slice.39, s32[512]{0:T(512)S(1)} %dynamic_slice.40, pred[]{:T(512)S(6)} %compare.19, bf16[512,2048]{1,0:T(8,128)(2,1)} %get-tuple-element.272, s32[]{:T(128)S(6)} %select_n.101), kind=kOutput, calls=%fused_computation.1.clone.1 | convolution fusion | flops 548462592 | bytes 4755461 | tf_op jit(solution)/shard_map/while/body/eval_jaxpr/dot_general | solution.py:53
  16.5 2.3 %collective-permute-start = (f32[512,4]{0,1:T(4,128)S(1)}, f32[512,4]{0,1:T(4,128)S(1)}, u32[]{:S(2)}, u32[]{:S(2)}) collective-permute-start(f32[512,4]{0,1:T(4,128)S(1)} %slice.58), channel_id=1, source_target_pairs={{0,8},{8,16},{16,24},{24,32},{32,40},{40,48},{48,56},{56,64},{64,7... | collective-permute-start | bytes 24584 | tf_op jit(solution)/shard_map/ppermute | solution.py:25
  18.8 0.6 compare_reduce_fusion
  19.4 0.2 collective-permute-done
  19.6 0.7 fusion.117
  20.3 0.1 copy.26
  20.4 6.0 %collective-permute-start.1 = (f32[512,4]{1,0:T(8,128)S(1)}, f32[512,4]{1,0:T(8,128)S(1)}, u32[]{:S(2)}, u32[]{:S(2)}) collective-permute-start(f32[512,4]{1,0:T(8,128)S(1)} %copy.26), channel_id=1, source_target_pairs={{8,0},{16,8},{24,16},{32,24},{40,32},{48,40},{56,48},{64,56},{72,6... | collective-permute-start | bytes 24584 | tf_op jit(solution)/shard_map/ppermute | solution.py:27
  26.4 1.9 copy.24
  28.3 2.3 %slice.63 = f32[512,1024]{1,0:T(8,128)S(1)} slice(f32[512,1032]{1,0:T(8,128)} %copy.24), slice={[0:512], [4:1028]} | slice | bytes 4194304 | tf_op jit(solution)/shard_map/slice | solution.py:120
  30.6 0.1 copy.25
  30.7 1.9 scatter-add.6
  32.7 0.0 collective-permute-done.1
  32.7 0.1 slice_add_fusion
  32.8 1.5 scatter-add.9
  34.3 0.2 convert_element_type.58
  34.5 1.1 copy.27
  35.5 33.6 %all_to_all.33 = bf16[2,1,256,1024]{3,0,1,2:T(2,128)(2,1)S(1)} all-to-all(bf16[2,1,256,1024]{3,0,1,2:T(2,128)(2,1)S(1)} %copy.27), channel_id=1, replica_groups=mesh['tm'=32,'freq'=8] {'tm'}, dimensions={2} | all-to-all | bytes 2097152 | tf_op jit(solution)/shard_map/all_to_all | solution.py:129
  69.1 0.3 copy.28
  69.4 25.2 %copy.29 = bf16[2,1,8,32768]{2,0,1,3:T(2,128)(2,1)} copy(bf16[2,1,8,32768]{3,2,0,1:T(8,128)(2,1)S(1)} %bitcast.89) | data formatting | bytes 2097152 | tf_op jit(solution)/shard_map/all_to_all | solution.py:129
  94.5 20.5 %reshape.173 = bf16[8,2,32768]{2,1,0:T(2,128)(2,1)} reshape(bf16[32768,1,2,8]{3,2,1,0:T(2,128)(2,1)} %bitcast.85) | data formatting | bytes 2097152
  115.0 5.3 %all-to-all-start.1 = ((bf16[8,2,32768]{2,1,0:T(2,128)(2,1)}), bf16[8,2,32768]{2,1,0:T(2,128)(2,1)S(1)}, u32[]{:S(2)}, u32[]{:S(2)}) async-start(bf16[8,2,32768]{2,1,0:T(2,128)(2,1)} %reshape.173), calls=%async_computation.1 | async-start | bytes 2097152 | tf_op jit(solution)/shard_map/all_to_all | solution.py:128
  120.3 0.1 fusion.74
  120.3 13.6 %all-to-all-done.1 = bf16[8,2,32768]{2,1,0:T(2,128)(2,1)S(1)} async-done(((bf16[8,2,32768]{2,1,0:T(2,128)(2,1)}), bf16[8,2,32768]{2,1,0:T(2,128)(2,1)S(1)}, u32[]{:S(2)}, u32[]{:S(2)}) %all-to-all-start.1) | async-done | bytes 1048608 | tf_op jit(solution)/shard_map/all_to_all | solution.py:128
  133.9 20.7 %reshape.174 = bf16[32768,1,2,8]{3,2,1,0:T(2,128)(2,1)} reshape(bf16[8,2,32768]{2,1,0:T(2,128)(2,1)S(1)} %all-to-all-done.1) | data formatting | bytes 2097152
  154.6 32.5 %copy.30 = bf16[2,1,8,8,4096]{4,2,3,1,0:T(8,128)(2,1)S(1)} copy(bf16[2,1,8,8,4096]{2,0,4,3,1:T(2,128)(2,1)} %bitcast.86) | data formatting | bytes 2097152 | tf_op jit(solution)/shard_map/all_to_all | solution.py:128
  187.1 0.1 slice_bitcast_fusion
  187.2 0.5 fusion.41
  187.7 0.5 fusion.45
  188.2 0.6 fusion.33
  188.8 0.5 fusion.34
  189.3 0.9 fusion.39
  190.2 0.9 fusion.35
  191.0 0.9 fusion.32
  191.9 0.9 fusion.31
  192.8 1.6 fusion.30
  (2 shorter events, 0.0 us)
Async XLA Ops:
  16.5 3.1 %collective-permute-start = (f32[512,4]{0,1:T(4,128)S(1)}, f32[512,4]{0,1:T(4,128)S(1)}, u32[]{:S(2)}, u32[]{:S(2)}) collective-permute-start(f32[512,4]{0,1:T(4,128)S(1)} %slice.58), channel_id=1, source_target_pairs={{0,8},{8,16},{16,24},{24,32},{32,40},{40,48},{48,56},{56,64},{64,7... | collective-permute-start | bytes 24584 | tf_op jit(solution)/shard_map/ppermute | solution.py:25
  20.4 12.2 %collective-permute-start.1 = (f32[512,4]{1,0:T(8,128)S(1)}, f32[512,4]{1,0:T(8,128)S(1)}, u32[]{:S(2)}, u32[]{:S(2)}) collective-permute-start(f32[512,4]{1,0:T(8,128)S(1)} %copy.26), channel_id=1, source_target_pairs={{8,0},{16,8},{24,16},{32,24},{40,32},{48,40},{56,48},{64,56},{72,6... | collective-permute-start | bytes 24584 | tf_op jit(solution)/shard_map/ppermute | solution.py:27
  115.0 18.9 %all-to-all-start.1 = ((bf16[8,2,32768]{2,1,0:T(2,128)(2,1)}), bf16[8,2,32768]{2,1,0:T(2,128)(2,1)S(1)}, u32[]{:S(2)}, u32[]{:S(2)}) async-start(bf16[8,2,32768]{2,1,0:T(2,128)(2,1)} %reshape.173), calls=%async_computation.1 | async-start | bytes 2097152 | tf_op jit(solution)/shard_map/all_to_all | solution.py:128
where the time goes:
time: 198 us; the launch traced here: 194 us
  local copies, waits for them, and re-layouts  111 us (56%)
  blocking collectives  33.6 us (17%)
  matrix products  17.9 us (9%)
  waiting for transfers between devices  13.8 us (7%)
  starting transfers between devices  13.5 us (7%)
  other arithmetic  3.95 us (2%)
    unnamed x3, local copies, waits for them, and re-layouts  41.2 us
    all_to_all x1, blocking collectives, shards(): lax.all_to_all(rounded, 'tm', split_axis=2, concat_axis=3, tiled=True)  33.6 us
    all_to_all x1, local copies, waits for them, and re-layouts, shards(): lax.all_to_all(lax.all_to_all(rounded, 'tm', split_axis=2, concat_axis=3,...  32.5 us
    all_to_all x2, local copies, waits for them, and re-layouts, shards(): lax.all_to_all(rounded, 'tm', split_axis=2, concat_axis=3, tiled=True)  25.4 us
    all_to_all x1, waiting for transfers between devices, shards(): lax.all_to_all(lax.all_to_all(rounded, 'tm', split_axis=2, concat_axis=3,...  13.6 us
    dot_general x4, matrix products, accumulate(): jnp.dot(sample_block, weight_table, preferred_element_type=jnp.float32)  12.4 us
    ppermute x1, starting transfers between devices, with_halo(): lax.ppermute(head, axis, [((i + 1) % count, i) for i in range(count)])  5.95 us
    all_to_all x1, starting transfers between devices, shards(): lax.all_to_all(lax.all_to_all(rounded, 'tm', split_axis=2, concat_axis=3,...  5.26 us
  transfers between devices with their start and end apart: 3, of which 2 were waited for; matrix products, arithmetic and copies ran while one was open for 4% of the time, Pallas kernels for 0%

commit v1 on v0

v1 whole, which is shorter than its diff:
```python
import math

import jax
import jax.numpy as jnp
import numpy as np
from jax import lax
from jax.experimental import pallas as pl
from jax.experimental.pallas import tpu as pltpu
from jax.sharding import PartitionSpec as P

TAPS = 8
GRID_DEV = 1024
FFT_LO = 32
FFT_HI = 128
FFTLEN = 4096
MESH = pl.DeviceIdType.MESH

sharpness = 0.3

CHUNKS = 4
CHUNK = GRID_DEV // CHUNKS
TILE = 16


def destination(step, block):
    ring, inner = step // 4, step % 4
    shift = ((ring + 1) // 2) * (2 * (ring % 2) - 1)
    half = (block // 16 + inner // 2) % 2
    return half * 16 + ((block // 2) % 8 + shift + 8) % 8 * 2 + (block + inner) % 2


def spread_kernel(
    strength_hbm,
    cell_ref,
    frac_ref,
    received,
    strength,
    window,
    outgoing,
    partial,
    halo,
    halo_in,
    load_sem,
    send_sem,
    recv_sem,
    halo_send_sem,
    halo_recv_sem,
):
    block = lax.axis_index("tm")
    group = lax.axis_index("freq")
    frame = block // 4
    blocks = 32
    right, left = (block + 1) % blocks, (block + blocks - 1) % blocks

    load = pltpu.make_async_copy(strength_hbm, strength, load_sem)
    load.start()

    barrier = pltpu.get_barrier_semaphore()

    def greet(i, carry):
        pl.semaphore_signal(
            barrier, inc=1, device_id=(4 * group + i // 8, i % 8), device_id_type=MESH
        )
        return carry

    lax.fori_loop(0, 32, greet, 0)
    for beside in (left, right):
        pl.semaphore_signal(barrier, inc=1, device_id=(beside, group), device_id_type=MESH)

    samples = cell_ref.shape[1]
    start = jnp.broadcast_to(
        cell_ref[...] - block * GRID_DEV + (TILE - (TAPS // 2 - 1)), (TILE, samples)
    )
    row = lax.broadcasted_iota(jnp.int32, (TILE, samples), 0)
    phase = start & (TILE - 1)
    tap = (row - phase) & (TILE - 1)
    shifted = tap.astype(jnp.float32) - float(TAPS // 2 - 1) - frac_ref[...]
    values = jnp.exp(-sharpness * (shifted * shifted))
    values = jnp.where(tap < TAPS, values, 0.0).astype(jnp.bfloat16)
    tile_of = (lax.shift_right_logical(start, 4) + jnp.where(row < phase, 1, 0)).astype(
        jnp.float32
    )
    edge = jnp.where(row < TILE // 2, float(GRID_DEV // TILE + 1), 0.0)
    nothing = jnp.zeros_like(values)
    edge_window = jnp.where(tile_of == edge, values.astype(jnp.float32), 0.0).astype(jnp.bfloat16)
    tile_of = tile_of.astype(jnp.bfloat16)

    def build(chunk):
        for i in range(CHUNK // TILE):
            q = chunk * (CHUNK // TILE) + i
            window[q * TILE : (q + 1) * TILE, :] = jnp.where(
                tile_of == jnp.bfloat16(q + 1), values, nothing
            )

    across = (((1,), (1,)), ((), ()))

    def rows():
        return strength[...].reshape(2 * strength.shape[2], samples)

    def gather(chunk):
        return lax.dot_general(
            rows(),
            window[chunk * CHUNK : (chunk + 1) * CHUNK, :],
            across,
            preferred_element_type=jnp.float32,
        )

    def round_out(chunk, total):
        channels = total.shape[0] // 2
        real = total[:channels].reshape(blocks, 8, total.shape[1])
        imag = total[channels:].reshape(blocks, 8, total.shape[1])
        outgoing[chunk] = jnp.concatenate([real, imag], axis=1).astype(jnp.bfloat16)

    def send(chunk):
        def one(step, carry):
            target = destination(step, block)
            src = outgoing.at[chunk, target]
            dst = received.at[group, block % 4, chunk]
            own = jnp.logical_and(target == block, frame == group)

            @pl.when(jnp.logical_not(own))
            def _():
                pltpu.make_async_remote_copy(
                    src_ref=src,
                    dst_ref=dst,
                    send_sem=send_sem,
                    recv_sem=recv_sem,
                    device_id=(target, frame),
                    device_id_type=MESH,
                ).start()

            @pl.when(own)
            def _():
                pltpu.make_async_copy(src, dst, recv_sem).start()

            return carry

        lax.fori_loop(0, blocks, one, 0)

    build(1)
    load.wait()
    round_out(1, gather(1))
    pl.semaphore_wait(barrier, 34)
    send(1)

    halo[...] = lax.dot_general(edge_window, rows(), across, preferred_element_type=jnp.float32)
    to_right = pltpu.make_async_remote_copy(
        src_ref=halo.at[0:8],
        dst_ref=halo_in.at[0:8],
        send_sem=halo_send_sem,
        recv_sem=halo_recv_sem,
        device_id=(right, group),
        device_id_type=MESH,
    )
    to_left = pltpu.make_async_remote_copy(
        src_ref=halo.at[8:16],
        dst_ref=halo_in.at[120:128],
        send_sem=halo_send_sem,
        recv_sem=halo_recv_sem,
        device_id=(left, group),
        device_id_type=MESH,
    )
    to_right.start()
    to_left.start()

    build(2)
    round_out(2, gather(2))
    send(2)
    build(0)
    partial[0] = gather(0)
    build(3)
    partial[1] = gather(3)
    halo_in[8:120, :] = jnp.zeros((112, halo_in.shape[1]), jnp.float32)

    pltpu.make_async_copy(halo, halo_in.at[0:16], halo_recv_sem).wait()
    beyond = halo_in[...].T
    lane = lax.broadcasted_iota(jnp.int32, beyond.shape, 1)
    none = jnp.zeros((beyond.shape[0], CHUNK - 128), jnp.float32)
    round_out(
        0, partial[0] + jnp.concatenate([jnp.where(lane < 8, beyond, 0.0), none], axis=1)
    )
    send(0)
    round_out(
        3, partial[1] + jnp.concatenate([none, jnp.where(lane >= 120, beyond, 0.0)], axis=1)
    )
    send(3)

    pltpu.make_async_copy(halo, halo_in.at[0:16], halo_send_sem).wait()
    pltpu.make_async_copy(outgoing, received, recv_sem).wait()

    @pl.when(frame == group)
    def _():
        pltpu.make_async_copy(
            outgoing.at[:, 0:31], outgoing.at[:, 0:31], send_sem
        ).wait()

    @pl.when(frame != group)
    def _():
        pltpu.make_async_copy(outgoing, outgoing, send_sem).wait()


def spread(strengths, sample_cell, sample_frac):
    channels, samples = strengths.shape[2], strengths.shape[3]
    rows = 2 * channels
    return pl.pallas_call(
        spread_kernel,
        out_shape=jax.ShapeDtypeStruct((8, 4, CHUNKS, 16, CHUNK), jnp.bfloat16),
        in_specs=[
            pl.BlockSpec(memory_space=pl.ANY),
            pl.BlockSpec(memory_space=pltpu.VMEM),
            pl.BlockSpec(memory_space=pltpu.VMEM),
        ],
        out_specs=pl.BlockSpec(memory_space=pl.ANY),
        scratch_shapes=[
            pltpu.VMEM(strengths.shape, jnp.bfloat16),
            pltpu.VMEM((GRID_DEV, samples), jnp.bfloat16),
            pltpu.VMEM((CHUNKS, 32, 16, CHUNK), jnp.bfloat16),
            pltpu.VMEM((2, rows, CHUNK), jnp.float32),
            pltpu.VMEM((16, rows), jnp.float32),
            pltpu.VMEM((128, rows), jnp.float32),
            pltpu.SemaphoreType.DMA,
            pltpu.SemaphoreType.DMA,
            pltpu.SemaphoreType.DMA,
            pltpu.SemaphoreType.DMA,
            pltpu.SemaphoreType.DMA,
        ],
        compiler_params=pltpu.CompilerParams(
            collective_id=0, has_side_effects=True, vmem_limit_bytes=48 * 1024 * 1024
        ),
    )(strengths, sample_cell.reshape(1, samples), sample_frac.reshape(1, samples))


def split_bf16(table):
    high = table.astype(jnp.bfloat16)
    low = (table - high.astype(np.float64)).astype(jnp.bfloat16)
    return high, low


def transform_tables():
    digit = np.arange(16)
    angle = 2.0 * math.pi * (digit[:, None] * digit[None, :] % 16) / 16
    cos, sin, same = np.cos(angle), np.sin(angle), np.eye(8)

    def block(part):
        return np.einsum("am,cd->camd", part, same)

    first = np.zeros((2, 8, 16, 16, 2, 8))
    first[0, :, :, :, 0] = block(cos)
    first[0, :, :, :, 1] = block(sin)
    first[1, :, :, :, 0] = block(-sin)
    first[1, :, :, :, 1] = block(cos)
    first = first.reshape(256, 256)

    n = np.arange(FFT_HI)
    half_turn = 2.0 * math.pi * digit[:, None] / FFT_LO * np.ones((1, FFT_HI))
    turn = 2.0 * math.pi * np.arange(FFT_LO)[:, None] * n[None, :] / FFTLEN
    turns = np.stack(
        [
            np.cos(half_turn),
            np.sin(half_turn),
            np.cos(turn[:16]),
            np.sin(turn[:16]),
            np.cos(turn[16:]),
            np.sin(turn[16:]),
        ]
    ).astype(np.float32)

    angle = 2.0 * math.pi * (n[:, None] * n[None, :] % FFT_HI) / FFT_HI
    cos, sin = np.cos(angle), np.sin(angle)
    last = np.block([[cos, -sin], [sin, cos]]) / math.sqrt(FFTLEN)
    return split_bf16(first), turns, split_bf16(last)


def transform_kernel(data_ref, first_hi, first_lo, turns, last_hi, last_lo, out_ref):
    data = data_ref[...].reshape(256, 256)

    def dot(a, b):
        return jnp.dot(a, b, preferred_element_type=jnp.float32)

    def turned(real, imag, cos, sin):
        return real * cos + imag * sin, imag * cos - real * sin

    section = dot(first_hi[...], data) + dot(first_lo[...], data)
    section = section.reshape(2, 8, 16, 256)
    even_real, odd_real = section[0, :, :, :128], section[0, :, :, 128:]
    even_imag, odd_imag = section[1, :, :, :128], section[1, :, :, 128:]
    odd_real, odd_imag = turned(odd_real, odd_imag, turns[0], turns[1])
    halves = (
        turned(even_real + odd_real, even_imag + odd_imag, turns[2], turns[3]),
        turned(even_real - odd_real, even_imag - odd_imag, turns[4], turns[5]),
    )
    for half, (real, imag) in enumerate(halves):
        both = jnp.concatenate([real.reshape(128, 128), imag.reshape(128, 128)], axis=1)
        high = both.astype(jnp.bfloat16)
        low = (both - high.astype(jnp.float32)).astype(jnp.bfloat16)
        result = dot(high, last_hi[...]) + dot(low, last_hi[...]) + dot(high, last_lo[...])
        for part in range(2):
            out_ref[part, 0, :, 0, half * 16 : half * 16 + 16, :] = result[
                :, part * 128 : (part + 1) * 128
            ].reshape(8, 16, 128)


def transform(received):
    (first_hi, first_lo), turns, (last_hi, last_lo) = transform_tables()
    table = pl.BlockSpec((256, 256), lambda g: (0, 0))
    return pl.pallas_call(
        transform_kernel,
        grid=(8,),
        out_shape=jax.ShapeDtypeStruct((2, 8, 8, 1, FFT_LO, FFT_HI), jnp.float32),
        in_specs=[
            pl.BlockSpec((1, 4, CHUNKS, 16, CHUNK), lambda g: (g, 0, 0, 0, 0)),
            table,
            table,
            pl.BlockSpec((6, 16, 128), lambda g: (0, 0, 0)),
            table,
            table,
        ],
        out_specs=pl.BlockSpec((2, 1, 8, 1, FFT_LO, FFT_HI), lambda g: (0, g, 0, 0, 0, 0)),
    )(received, first_hi, first_lo, turns, last_hi, last_lo)


def shards(strengths, sample_cell, sample_frac):
    return transform(spread(strengths, sample_cell, sample_frac))


def solution(mesh):
    placed = (P(None, "freq", None, "tm"), P("tm"), P("tm"))
    return jax.shard_map(
        shards,
        mesh=mesh,
        in_specs=placed,
        out_specs=P(None, None, "tm", "freq", None, None),
        check_vma=False,
    )
```

time: 198 us -> 50.1 us (0.25); the launches traced: 194 us -> 49.7 us
  local copies, waits for them, and re-layouts: 111 us -> 3.94 us
  Pallas kernels: 0 us -> 45.8 us
  blocking collectives: 33.6 us -> 0 us
  matrix products: 17.9 us -> 0 us
  waiting for transfers between devices: 13.8 us -> 0 us
  starting transfers between devices: 13.5 us -> 0 us
  other arithmetic: 3.95 us -> 0 us
    all_to_all x3 -> x0, local copies, waits for them, and re-layouts: 57.9 us -> none  [the longest x1 32.5 us: shards(): lax.all_to_all(lax.all_to_all(rounded, 'tm', split_axis=2, concat_axis=3,...]
    pallas_call x0 -> x2, Pallas kernels: none -> 45.8 us  [the longest x1 37.9 us: spread(): pl.pallas_call(spread_kernel, out_shape=jax.ShapeDtypeStruct((8, 4, CHUNK...]
    unnamed x3 -> x8, local copies, waits for them, and re-layouts: 41.2 us -> 3.94 us
    all_to_all x1 -> x0, blocking collectives: 33.6 us -> none  [shards(): lax.all_to_all(rounded, 'tm', split_axis=2, concat_axis=3, tiled=True)]
    dot_general x12 -> x0, matrix products: 17.9 us -> none  [the longest x4 12.4 us: accumulate(): jnp.dot(sample_block, weight_table, preferred_element_type=jnp.float32)]
    all_to_all x1 -> x0, waiting for transfers between devices: 13.6 us -> none  [shards(): lax.all_to_all(lax.all_to_all(rounded, 'tm', split_axis=2, concat_axis=3,...]
    ppermute x2 -> x0, starting transfers between devices: 8.23 us -> none  [the longest x1 5.95 us: with_halo(): lax.ppermute(head, axis, [((i + 1) % count, i) for i in range(count)])]
    all_to_all x1 -> x0, starting transfers between devices: 5.26 us -> none  [shards(): lax.all_to_all(lax.all_to_all(rounded, 'tm', split_axis=2, concat_axis=3,...]
  transfers between devices with their start and end apart: 3 -> 0, of which waited for: 2 -> 0; matrix products, arithmetic and copies ran while one was open for 4% -> 0% of each run, Pallas kernels for 0% -> 0%
where the time goes in v1:
time: 50.1 us; the launch traced here: 49.7 us
  Pallas kernels  45.8 us (91%)
  local copies, waits for them, and re-layouts  3.94 us (8%)
    pallas_call x1, Pallas kernels, spread(): pl.pallas_call(spread_kernel, out_shape=jax.ShapeDtypeStruct((8, 4, CHUNK...  37.9 us
    pallas_call x1, Pallas kernels, transform(): pl.pallas_call(transform_kernel, grid=(8,), out_shape=jax.ShapeDtypeStruc...  7.85 us
    unnamed x8, local copies, waits for them, and re-layouts  3.94 us

profile of v1, /device:TPU:11, one launch (start us, length us, event | category | flops | bytes accessed | tf_op | source)
XLA Modules:
  0.0 49.7 jit_solution(464583937390490871)
XLA Ops:
  0.0 0.0 copy-start.1
  0.0 1.6 %copy-done.1 = bf16[2,1,256,2048]{3,2,1,0:T(8,128)(2,1)S(1)} copy-done((bf16[2,1,256,2048]{3,2,1,0:T(8,128)(2,1)S(1)}, bf16[2,1,256,2048]{3,2,1,0:T(8,128)(2,1)}, u32[]{:S(2)}) %copy-start.1) | copy-done | bytes 2097176
  1.6 0.0 copy-start.2
  1.6 0.7 %copy-done.2 = s32[2048]{0:T(1024)S(1)} copy-done((s32[2048]{0:T(1024)S(1)}, s32[2048]{0:T(1024)}, u32[]{:S(2)}) %copy-start.2) | copy-done | bytes 8216
  2.3 0.0 copy-start.3
  2.3 0.7 %copy-done.3 = f32[2048]{0:T(1024)S(1)} copy-done((f32[2048]{0:T(1024)S(1)}, f32[2048]{0:T(1024)}, u32[]{:S(2)}) %copy-start.3) | copy-done | bytes 8216
  3.0 37.9 %shard_map.82.data_ref = bf16[8,4,4,16,256]{4,3,2,1,0:T(8,128)(2,1)S(1)} custom-call(bf16[2,1,256,2048]{3,2,1,0:T(8,128)(2,1)S(1)} %copy-done.1, s32[1,2048]{1,0:T(1,128)S(1)} %bitcast.2, f32[1,2048]{1,0:T(1,128)S(1)} %bitcast.3), custom_call_target="tpu_custom_call" | custom-call | tf_op jit(solution)/shard_map/pallas_call | solution.py:205
  40.9 0.0 copy-start
  40.9 1.0 %copy-done = bf16[8,4,4,16,256]{4,3,2,1,0:T(8,128)(2,1)} copy-done((bf16[8,4,4,16,256]{4,3,2,1,0:T(8,128)(2,1)}, bf16[8,4,4,16,256]{4,3,2,1,0:T(8,128)(2,1)S(1)}, u32[]{:S(2)}) %copy-start) | copy-done | bytes 1048600
  41.9 7.8 %shard_map.83 = f32[2,8,8,1,32,128]{5,4,3,2,1,0:T(8,128)} custom-call(bf16[8,4,4,16,256]{4,3,2,1,0:T(8,128)(2,1)} %copy-done, bf16[256,256]{1,0:T(8,128)(2,1)} %constant.10.clone.first_hi, bf16[256,256]{1,0:T(8,128)(2,1)} %constant.11.clone.first_lo, f32[6,16,128]{2,1,0:T(8,128)} %constant.12.clone.turns, bf16[256,256]{1,0:T(8,128)(2,1)} %constant.13.clone.last_hi, ...), custom_call_target="tpu_custom_call" | custom-call | tf_op jit(solution)/shard_map/pallas_call | solution.py:306
Async XLA Ops:
  0.0 1.6 %copy-start.1 = (bf16[2,1,256,2048]{3,2,1,0:T(8,128)(2,1)S(1)}, bf16[2,1,256,2048]{3,2,1,0:T(8,128)(2,1)}, u32[]{:S(2)}) copy-start(bf16[2,1,256,2048]{3,2,1,0:T(8,128)(2,1)} %strength_hbm.1) | copy-start | bytes 6291460
  1.6 0.7 %copy-start.2 = (s32[2048]{0:T(1024)S(1)}, s32[2048]{0:T(1024)}, u32[]{:S(2)}) copy-start(s32[2048]{0:T(1024)} %param.9) | copy-start | bytes 24580
  2.3 0.7 %copy-start.3 = (f32[2048]{0:T(1024)S(1)}, f32[2048]{0:T(1024)}, u32[]{:S(2)}) copy-start(f32[2048]{0:T(1024)} %param.10) | copy-start | bytes 24580
  40.9 1.0 %copy-start = (bf16[8,4,4,16,256]{4,3,2,1,0:T(8,128)(2,1)}, bf16[8,4,4,16,256]{4,3,2,1,0:T(8,128)(2,1)S(1)}, u32[]{:S(2)}) copy-start(bf16[8,4,4,16,256]{4,3,2,1,0:T(8,128)(2,1)S(1)} %shard_map.82.data_ref) | copy-start | bytes 3145732

commit v2 on v1

--- a/solution.py
+++ b/solution.py
@@ -31,9 +31,11 @@
 
 def spread_kernel(
     strength_hbm,
+    cell_hbm,
+    frac_hbm,
+    received,
     cell_ref,
     frac_ref,
-    received,
     strength,
     window,
     outgoing,
@@ -52,8 +54,13 @@
     blocks = 32
     right, left = (block + 1) % blocks, (block + blocks - 1) % blocks
 
-    load = pltpu.make_async_copy(strength_hbm, strength, load_sem)
-    load.start()
+    loads = [
+        pltpu.make_async_copy(cell_hbm, cell_ref, load_sem.at[0]),
+        pltpu.make_async_copy(frac_hbm, frac_ref, load_sem.at[1]),
+        pltpu.make_async_copy(strength_hbm, strength, load_sem.at[2]),
+    ]
+    for load in loads:
+        load.start()
 
     barrier = pltpu.get_barrier_semaphore()
 
@@ -67,6 +74,8 @@
     for beside in (left, right):
         pl.semaphore_signal(barrier, inc=1, device_id=(beside, group), device_id_type=MESH)
 
+    loads[0].wait()
+    loads[1].wait()
     samples = cell_ref.shape[1]
     start = jnp.broadcast_to(
         cell_ref[...] - block * GRID_DEV + (TILE - (TAPS // 2 - 1)), (TILE, samples)
@@ -138,7 +147,7 @@
         lax.fori_loop(0, blocks, one, 0)
 
     build(1)
-    load.wait()
+    loads[2].wait()
     round_out(1, gather(1))
     pl.semaphore_wait(barrier, 34)
     send(1)
@@ -205,20 +214,18 @@
     return pl.pallas_call(
         spread_kernel,
         out_shape=jax.ShapeDtypeStruct((8, 4, CHUNKS, 16, CHUNK), jnp.bfloat16),
-        in_specs=[
-            pl.BlockSpec(memory_space=pl.ANY),
-            pl.BlockSpec(memory_space=pltpu.VMEM),
-            pl.BlockSpec(memory_space=pltpu.VMEM),
-        ],
-        out_specs=pl.BlockSpec(memory_space=pl.ANY),
+        in_specs=[pl.BlockSpec(memory_space=pltpu.HBM)] * 3,
+        out_specs=pl.BlockSpec(memory_space=pltpu.VMEM),
         scratch_shapes=[
+            pltpu.VMEM((1, samples), jnp.int32),
+            pltpu.VMEM((1, samples), jnp.float32),
             pltpu.VMEM(strengths.shape, jnp.bfloat16),
             pltpu.VMEM((GRID_DEV, samples), jnp.bfloat16),
             pltpu.VMEM((CHUNKS, 32, 16, CHUNK), jnp.bfloat16),
             pltpu.VMEM((2, rows, CHUNK), jnp.float32),
             pltpu.VMEM((16, rows), jnp.float32),
             pltpu.VMEM((128, rows), jnp.float32),
-            pltpu.SemaphoreType.DMA,
+            pltpu.SemaphoreType.DMA((3,)),
             pltpu.SemaphoreType.DMA,
             pltpu.SemaphoreType.DMA,
             pltpu.SemaphoreType.DMA,
@@ -227,7 +234,12 @@
         compiler_params=pltpu.CompilerParams(
             collective_id=0, has_side_effects=True, vmem_limit_bytes=48 * 1024 * 1024
         ),
-    )(strengths, sample_cell.reshape(1, samples), sample_frac.reshape(1, samples))
+    )(
+        *(
+            pltpu.with_memory_space_constraint(x, pltpu.HBM)
+            for x in (strengths, sample_cell.reshape(1, samples), sample_frac.reshape(1, samples))
+        )
+    )
 
 
 def split_bf16(table):
@@ -271,51 +283,62 @@
     return split_bf16(first), turns, split_bf16(last)
 
 
-def transform_kernel(data_ref, first_hi, first_lo, turns, last_hi, last_lo, out_ref):
-    data = data_ref[...].reshape(256, 256)
-
+def transform_kernel(data_ref, first_hi, first_lo, turns, last_hi, last_lo, out_hbm, out, sem):
     def dot(a, b):
         return jnp.dot(a, b, preferred_element_type=jnp.float32)
 
     def turned(real, imag, cos, sin):
         return real * cos + imag * sin, imag * cos - real * sin
 
-    section = dot(first_hi[...], data) + dot(first_lo[...], data)
-    section = section.reshape(2, 8, 16, 256)
-    even_real, odd_real = section[0, :, :, :128], section[0, :, :, 128:]
-    even_imag, odd_imag = section[1, :, :, :128], section[1, :, :, 128:]
-    odd_real, odd_imag = turned(odd_real, odd_imag, turns[0], turns[1])
-    halves = (
-        turned(even_real + odd_real, even_imag + odd_imag, turns[2], turns[3]),
-        turned(even_real - odd_real, even_imag - odd_imag, turns[4], turns[5]),
-    )
-    for half, (real, imag) in enumerate(halves):
-        both = jnp.concatenate([real.reshape(128, 128), imag.reshape(128, 128)], axis=1)
+    def store(group):
+        return pltpu.make_async_copy(out.at[group], out_hbm.at[:, group, :, 0], sem)
+
+    groups = data_ref.shape[0]
+    for group in range(groups):
+        data = data_ref[group].reshape(256, 256)
+        section = dot(first_hi[...], data) + dot(first_lo[...], data)
+        section = section.reshape(2, 8, 16, 256)
+        even_real, odd_real = section[0, :, :, :128], section[0, :, :, 128:]
+        even_imag, odd_imag = section[1, :, :, :128], section[1, :, :, 128:]
+        odd_real, odd_imag = turned(odd_real, odd_imag, turns[0], turns[1])
+        halves = (
+            turned(even_real + odd_real, even_imag + odd_imag, turns[2], turns[3]),
+            turned(even_real - odd_real, even_imag - odd_imag, turns[4], turns[5]),
+        )
+        both = jnp.concatenate(
+            [
+                jnp.concatenate([real.reshape(128, 128), imag.reshape(128, 128)], axis=1)
+                for real, imag in halves
+            ],
+            axis=0,
+        )
         high = both.astype(jnp.bfloat16)
         low = (both - high.astype(jnp.float32)).astype(jnp.bfloat16)
         result = dot(high, last_hi[...]) + dot(low, last_hi[...]) + dot(high, last_lo[...])
-        for part in range(2):
-            out_ref[part, 0, :, 0, half * 16 : half * 16 + 16, :] = result[
-                :, part * 128 : (part + 1) * 128
-            ].reshape(8, 16, 128)
+        for half in range(2):
+            for part in range(2):
+                out[group, part, :, half * 16 : half * 16 + 16, :] = result[
+                    half * 128 : (half + 1) * 128, part * 128 : (part + 1) * 128
+                ].reshape(8, 16, 128)
+        if group > 0:
+            store(group - 1).start()
+    store(groups - 1).start()
+    for group in range(groups):
+        store(group).wait()
 
 
 def transform(received):
     (first_hi, first_lo), turns, (last_hi, last_lo) = transform_tables()
-    table = pl.BlockSpec((256, 256), lambda g: (0, 0))
     return pl.pallas_call(
         transform_kernel,
-        grid=(8,),
         out_shape=jax.ShapeDtypeStruct((2, 8, 8, 1, FFT_LO, FFT_HI), jnp.float32),
-        in_specs=[
-            pl.BlockSpec((1, 4, CHUNKS, 16, CHUNK), lambda g: (g, 0, 0, 0, 0)),
-            table,
-            table,
-            pl.BlockSpec((6, 16, 128), lambda g: (0, 0, 0)),
-            table,
-            table,
+        in_specs=[pl.BlockSpec(memory_space=pltpu.VMEM)] * 6,
+        out_specs=pl.BlockSpec(memory_space=pltpu.HBM),
+        scratch_shapes=[
+            pltpu.VMEM((8, 2, 8, FFT_LO, FFT_HI), jnp.float32),
+            pltpu.SemaphoreType.DMA,
         ],
-        out_specs=pl.BlockSpec((2, 1, 8, 1, FFT_LO, FFT_HI), lambda g: (0, g, 0, 0, 0, 0)),
+        compiler_params=pltpu.CompilerParams(vmem_limit_bytes=32 * 1024 * 1024),
     )(received, first_hi, first_lo, turns, last_hi, last_lo)
 
 

time: 50.1 us -> 41.3 us (0.82)
  Pallas kernels: 45.8 us -> 41.1 us
  local copies, waits for them, and re-layouts: 3.94 us -> 0.02 us
    pallas_call x1, Pallas kernels: 7.85 us -> 3.08 us  [transform(): pl.pallas_call(transform_kernel, out_shape=jax.ShapeDtypeStruct((2, 8, 8,...]
    unnamed x8 -> x10, local copies, waits for them, and re-layouts: 3.94 us -> 0.02 us
where the time goes in v2:
time: 41.3 us; the launch traced here: 41.2 us
  Pallas kernels  41.1 us (100%)
    pallas_call x1, Pallas kernels, spread(): pl.pallas_call(spread_kernel, out_shape=jax.ShapeDtypeStruct((8, 4, CHUNK...  38 us
    pallas_call x1, Pallas kernels, transform(): pl.pallas_call(transform_kernel, out_shape=jax.ShapeDtypeStruct((2, 8, 8,...  3.08 us

profile of v2, /device:TPU:11, one launch (start us, length us, event | category | flops | bytes accessed | tf_op | source)
XLA Modules:
  0.0 41.2 jit_solution(5098903637158773945)
XLA Ops:
  0.0 0.0 copy-start
  0.0 0.0 copy-start.1
  0.0 0.0 copy-start.4
  0.0 0.0 copy-start.2
  0.0 0.0 copy-start.3
  0.0 38.0 %shard_map.82.data_ref = bf16[8,4,4,16,256]{4,3,2,1,0:T(8,128)(2,1)S(1)} custom-call(bf16[2,1,256,2048]{3,2,1,0:T(8,128)(2,1)} %strength_hbm.1, s32[1,2048]{1,0:T(1,128)} %bitcast.2, f32[1,2048]{1,0:T(1,128)} %bitcast.3), custom_call_target="tpu_custom_call" | custom-call | tf_op jit(solution)/shard_map/pallas_call | solution.py:214
  38.0 0.0 copy-done
  38.0 0.0 copy-done.1
  38.0 0.0 copy-done.4
  38.0 0.0 copy-done.2
  38.1 0.0 copy-done.3
  38.1 3.1 %shard_map.83 = f32[2,8,8,1,32,128]{5,4,3,2,1,0:T(8,128)} custom-call(bf16[8,4,4,16,256]{4,3,2,1,0:T(8,128)(2,1)S(1)} %shard_map.82.data_ref, bf16[256,256]{1,0:T(8,128)(2,1)S(1)} %copy-done.3, bf16[256,256]{1,0:T(8,128)(2,1)S(1)} %copy-done.2, f32[6,16,128]{2,1,0:T(8,128)S(1)} %copy-done.4, bf16[256,256]{1,0:T(8,128)(2,1)S(1)} %copy-done.1, ...), custom_call_target="tpu_custom_call" | custom-call | tf_op jit(solution)/shard_map/pallas_call | solution.py:332
Async XLA Ops:
  0.0 38.0 %copy-start = (bf16[256,256]{1,0:T(8,128)(2,1)S(1)}, bf16[256,256]{1,0:T(8,128)(2,1)}, u32[]{:S(2)}) copy-start(bf16[256,256]{1,0:T(8,128)(2,1)} %constant.14.clone.last_lo) | copy-start | bytes 393220
  0.0 38.0 %copy-start.1 = (bf16[256,256]{1,0:T(8,128)(2,1)S(1)}, bf16[256,256]{1,0:T(8,128)(2,1)}, u32[]{:S(2)}) copy-start(bf16[256,256]{1,0:T(8,128)(2,1)} %constant.13.clone.last_hi) | copy-start | bytes 393220
  0.0 38.0 %copy-start.4 = (f32[6,16,128]{2,1,0:T(8,128)S(1)}, f32[6,16,128]{2,1,0:T(8,128)}, u32[]{:S(2)}) copy-start(f32[6,16,128]{2,1,0:T(8,128)} %constant.12.clone.turns) | copy-start | bytes 147460
  0.0 38.0 %copy-start.2 = (bf16[256,256]{1,0:T(8,128)(2,1)S(1)}, bf16[256,256]{1,0:T(8,128)(2,1)}, u32[]{:S(2)}) copy-start(bf16[256,256]{1,0:T(8,128)(2,1)} %constant.11.clone.first_lo) | copy-start | bytes 393220
  0.0 38.0 %copy-start.3 = (bf16[256,256]{1,0:T(8,128)(2,1)S(1)}, bf16[256,256]{1,0:T(8,128)(2,1)}, u32[]{:S(2)}) copy-start(bf16[256,256]{1,0:T(8,128)(2,1)} %constant.10.clone.first_hi) | copy-start | bytes 393220

commit v3 on v2

v3 whole, which is shorter than its diff:
```python
import math

import jax
import jax.numpy as jnp
import numpy as np
from jax import lax
from jax.experimental import pallas as pl
from jax.experimental.pallas import tpu as pltpu
from jax.sharding import PartitionSpec as P

TAPS = 8
GRID_DEV = 1024
FFT_LO = 32
FFT_HI = 128
FFTLEN = 4096
MESH = pl.DeviceIdType.MESH

sharpness = 0.3

BLOCKS = 32
CHUNKS = 4
CHUNK = GRID_DEV // CHUNKS
TILE = 16
HALVES = 2
PAIRS = 4
MESSAGE = (8, CHUNK)


def plane(step, own):
    shift = ((step + 1) >> 1) * (2 * (step & 1) - 1)
    return (own + shift + 8) & 7


def transform_pair(data, first_hi, first_lo, turns, last_hi, last_lo):
    def dot(a, b):
        return jnp.dot(a, b, preferred_element_type=jnp.float32)

    def turned(real, imag, cos, sin):
        return real * cos + imag * sin, imag * cos - real * sin

    section = dot(first_hi[...], data) + dot(first_lo[...], data)
    section = section.reshape(2, 8, 16, 256)
    even_real, odd_real = section[0, :, :, :128], section[0, :, :, 128:]
    even_imag, odd_imag = section[1, :, :, :128], section[1, :, :, 128:]
    odd_real, odd_imag = turned(odd_real, odd_imag, turns[0], turns[1])
    halves = (
        turned(even_real + odd_real, even_imag + odd_imag, turns[2], turns[3]),
        turned(even_real - odd_real, even_imag - odd_imag, turns[4], turns[5]),
    )
    both = jnp.concatenate(
        [
            jnp.concatenate([real.reshape(128, 128), imag.reshape(128, 128)], axis=1)
            for real, imag in halves
        ],
        axis=0,
    )
    high = both.astype(jnp.bfloat16)
    return dot(high, last_hi[...]) + dot(high, last_lo[...])


def store_pair(out, pair, result):
    for half in range(2):
        for part in range(2):
            out[pair, part, :, :, half * 16 : half * 16 + 16, :] = result[
                half * 128 : (half + 1) * 128, part * 128 : (part + 1) * 128
            ].reshape(2, 4, 16, 128)


def spread_kernel(
    strength_hbm,
    cell_hbm,
    frac_hbm,
    first_hi_hbm,
    first_lo_hbm,
    turns_hbm,
    last_hi_hbm,
    last_lo_hbm,
    second,
    spectra,
    cell_ref,
    frac_ref,
    strength,
    window,
    outgoing,
    first,
    partial,
    halo,
    halo_in,
    first_hi,
    first_lo,
    turns,
    last_hi,
    last_lo,
    load_sem,
    table_sem,
    send_sem,
    recv_sem,
    halo_send_sem,
    halo_recv_sem,
):
    block = lax.axis_index("tm")
    group = lax.axis_index("freq")
    frame = block // 4
    right, left = (block + 1) % BLOCKS, (block + BLOCKS - 1) % BLOCKS

    loads = [
        pltpu.make_async_copy(cell_hbm, cell_ref, load_sem.at[0]),
        pltpu.make_async_copy(frac_hbm, frac_ref, load_sem.at[1]),
        pltpu.make_async_copy(strength_hbm, strength, load_sem.at[2]),
    ]
    for load in loads:
        load.start()

    barrier = pltpu.get_barrier_semaphore()

    def greet(i, carry):
        pl.semaphore_signal(
            barrier, inc=1, device_id=(4 * group + (i >> 3), i & 7), device_id_type=MESH
        )
        return carry

    lax.fori_loop(0, BLOCKS, greet, 0)
    for beside in (left, right):
        pl.semaphore_signal(barrier, inc=1, device_id=(beside, group), device_id_type=MESH)

    tables = [
        pltpu.make_async_copy(src, dst, table_sem.at[i])
        for i, (src, dst) in enumerate(
            (
                (first_hi_hbm, first_hi),
                (first_lo_hbm, first_lo),
                (turns_hbm, turns),
                (last_hi_hbm, last_hi),
                (last_lo_hbm, last_lo),
            )
        )
    ]
    for table in tables:
        table.start()

    loads[0].wait()
    loads[1].wait()
    samples = cell_ref.shape[1]
    start = jnp.broadcast_to(
        cell_ref[...] - block * GRID_DEV + (TILE - (TAPS // 2 - 1)), (TILE, samples)
    )
    row = lax.broadcasted_iota(jnp.int32, (TILE, samples), 0)
    phase = start & (TILE - 1)
    tap = (row - phase) & (TILE - 1)
    shifted = tap.astype(jnp.float32) - float(TAPS // 2 - 1) - frac_ref[...]
    values = jnp.exp(-sharpness * (shifted * shifted))
    values = jnp.where(tap < TAPS, values, 0.0).astype(jnp.bfloat16)
    tile_of = (lax.shift_right_logical(start, 4) + jnp.where(row < phase, 1, 0)).astype(
        jnp.float32
    )
    edge = jnp.where(row < TILE // 2, float(GRID_DEV // TILE + 1), 0.0)
    nothing = jnp.zeros_like(values)
    edge_window = jnp.where(tile_of == edge, values.astype(jnp.float32), 0.0).astype(jnp.bfloat16)
    tile_of = tile_of.astype(jnp.bfloat16)

    def build(chunk):
        for i in range(CHUNK // TILE):
            q = chunk * (CHUNK // TILE) + i
            window[q * TILE : (q + 1) * TILE, :] = jnp.where(
                tile_of == jnp.bfloat16(q + 1), values, nothing
            )

    across = (((1,), (1,)), ((), ()))

    def rows():
        return strength[...].reshape(2 * strength.shape[2], samples)

    def gather(chunk):
        return lax.dot_general(
            rows(),
            window[chunk * CHUNK : (chunk + 1) * CHUNK, :],
            across,
            preferred_element_type=jnp.float32,
        )

    def round_out(chunk, total):
        channels = total.shape[0] // 2
        real = total[:channels].reshape(BLOCKS, 8, CHUNK)
        imag = total[channels:].reshape(BLOCKS, 8, CHUNK)
        upper = lax.broadcasted_iota(jnp.int32, real.shape, 1) < 4
        outgoing[0, :, chunk] = jnp.where(upper, real, pltpu.roll(imag, 4, 1)).astype(jnp.bfloat16)
        outgoing[1, :, chunk] = jnp.where(upper, pltpu.roll(real, 4, 1), imag).astype(jnp.bfloat16)

    own_plane = (block >> 1) & 7
    offsets = [
        (((block >> 4) + (inner >> 1)) & 1) * 16 + ((block + inner) & 1) for inner in range(4)
    ]

    def send(half, begin, count):
        landing = (first, second)[half]
        dst = landing.at[group // 2, block % 4, group % 2, pl.ds(begin, count)]

        def one(step, carry):
            position = plane(step, own_plane)
            for inner in range(4):
                target = offsets[inner] + 2 * position
                src = outgoing.at[half, target, pl.ds(begin, count)]
                remote = pltpu.make_async_remote_copy(
                    src_ref=src,
                    dst_ref=dst,
                    send_sem=send_sem,
                    recv_sem=recv_sem.at[half],
                    device_id=(target, frame),
                    device_id_type=MESH,
                )
                if inner:
                    remote.start()
                    continue
                own = jnp.logical_and(position == own_plane, frame == group)

                @pl.when(jnp.logical_not(own))
                def _():
                    remote.start()

                @pl.when(own)
                def _():
                    pltpu.make_async_copy(src, dst, recv_sem.at[half]).start()

            return carry

        lax.fori_loop(0, 8, one, 0)

    build(1)
    loads[2].wait()
    round_out(1, gather(1))
    build(2)
    round_out(2, gather(2))
    halo[...] = lax.dot_general(edge_window, rows(), across, preferred_element_type=jnp.float32)

    pl.semaphore_wait(barrier, 34)
    to_right = pltpu.make_async_remote_copy(
        src_ref=halo.at[0:8],
        dst_ref=halo_in.at[0:8],
        send_sem=halo_send_sem,
        recv_sem=halo_recv_sem,
        device_id=(right, group),
        device_id_type=MESH,
    )
    to_left = pltpu.make_async_remote_copy(
        src_ref=halo.at[8:16],
        dst_ref=halo_in.at[120:128],
        send_sem=halo_send_sem,
        recv_sem=halo_recv_sem,
        device_id=(left, group),
        device_id_type=MESH,
    )
    to_right.start()
    to_left.start()
    send(0, 1, 2)

    build(0)
    partial[0] = gather(0)
    build(3)
    partial[1] = gather(3)
    halo_in[8:120, :] = jnp.zeros((112, halo_in.shape[1]), jnp.float32)

    pltpu.make_async_copy(halo, halo_in.at[0:16], halo_recv_sem).wait()
    beyond = halo_in[...].T
    lane = lax.broadcasted_iota(jnp.int32, beyond.shape, 1)
    none = jnp.zeros((beyond.shape[0], CHUNK - 128), jnp.float32)
    round_out(
        0, partial[0] + jnp.concatenate([jnp.where(lane < 8, beyond, 0.0), none], axis=1)
    )
    send(0, 0, 1)
    round_out(
        3, partial[1] + jnp.concatenate([none, jnp.where(lane >= 120, beyond, 0.0)], axis=1)
    )
    send(0, 3, 1)
    send(1, 0, 4)

    for table in tables:
        table.wait()
    pltpu.make_async_copy(outgoing.at[0], first, recv_sem.at[0]).wait()

    def one_pair(pair, carry):
        data = first[pair].reshape(256, 256)
        store_pair(
            spectra, pair, transform_pair(data, first_hi, first_lo, turns, last_hi, last_lo)
        )
        return carry

    lax.fori_loop(0, PAIRS, one_pair, 0)

    pltpu.make_async_copy(halo, halo_in.at[0:16], halo_send_sem).wait()

    @pl.when(frame == group)
    def _():
        pltpu.make_async_copy(outgoing.at[:, 0:31], outgoing.at[:, 0:31], send_sem).wait()

    @pl.when(frame != group)
    def _():
        pltpu.make_async_copy(outgoing, outgoing, send_sem).wait()

    pltpu.make_async_copy(outgoing.at[1], second, recv_sem.at[1]).wait()


def spread(strengths, sample_cell, sample_frac, tables):
    channels, samples = strengths.shape[2], strengths.shape[3]
    rows = 2 * channels
    half_shape = (PAIRS, 4, 2, CHUNKS, *MESSAGE)
    inputs = (
        strengths,
        sample_cell.reshape(1, samples),
        sample_frac.reshape(1, samples),
        *tables,
    )
    return pl.pallas_call(
        spread_kernel,
        out_shape=(
            jax.ShapeDtypeStruct(half_shape, jnp.bfloat16),
            jax.ShapeDtypeStruct((PAIRS, 2, 2, 4, FFT_LO, FFT_HI), jnp.float32),
        ),
        in_specs=[pl.BlockSpec(memory_space=pltpu.HBM)] * len(inputs),
        out_specs=(pl.BlockSpec(memory_space=pltpu.VMEM),) * 2,
        scratch_shapes=[
            pltpu.VMEM((1, samples), jnp.int32),
            pltpu.VMEM((1, samples), jnp.float32),
            pltpu.VMEM(strengths.shape, jnp.bfloat16),
            pltpu.VMEM((GRID_DEV, samples), jnp.bfloat16),
            pltpu.VMEM((HALVES, BLOCKS, CHUNKS, *MESSAGE), jnp.bfloat16),
            pltpu.VMEM(half_shape, jnp.bfloat16),
            pltpu.VMEM((2, rows, CHUNK), jnp.float32),
            pltpu.VMEM((16, rows), jnp.float32),
            pltpu.VMEM((128, rows), jnp.float32),
            *(pltpu.VMEM(table.shape, table.dtype) for table in tables),
            pltpu.SemaphoreType.DMA((3,)),
            pltpu.SemaphoreType.DMA((5,)),
            pltpu.SemaphoreType.DMA,
            pltpu.SemaphoreType.DMA((2,)),
            pltpu.SemaphoreType.DMA,
            pltpu.SemaphoreType.DMA,
        ],
        compiler_params=pltpu.CompilerParams(
            collective_id=0, has_side_effects=True, vmem_limit_bytes=48 * 1024 * 1024
        ),
    )(*(pltpu.with_memory_space_constraint(x, pltpu.HBM) for x in inputs))


def split_bf16(table):
    high = table.astype(jnp.bfloat16)
    low = (table - high.astype(np.float64)).astype(jnp.bfloat16)
    return high, low


def transform_tables():
    digit = np.arange(16)
    angle = 2.0 * math.pi * (digit[:, None] * digit[None, :] % 16) / 16
    cos, sin = np.cos(angle), np.sin(angle)
    group, channel = np.eye(2), np.eye(4)

    def entry(part):
        return np.einsum("atm,gh,cd->gcathmd", part.reshape(16, 4, 4), group, channel)

    first = np.zeros((2, 2, 4, 16, 4, 2, 4, 2, 4))
    first[0, ..., 0, :] = entry(cos)
    first[0, ..., 1, :] = entry(sin)
    first[1, ..., 0, :] = entry(-sin)
    first[1, ..., 1, :] = entry(cos)
    first = first.reshape(256, 256)

    n = np.arange(FFT_HI)
    half_turn = 2.0 * math.pi * digit[:, None] / FFT_LO * np.ones((1, FFT_HI))
    turn = 2.0 * math.pi * np.arange(FFT_LO)[:, None] * n[None, :] / FFTLEN
    turns = np.stack(
        [
            np.cos(half_turn),
            np.sin(half_turn),
            np.cos(turn[:16]),
            np.sin(turn[:16]),
            np.cos(turn[16:]),
            np.sin(turn[16:]),
        ]
    ).astype(np.float32)

    angle = 2.0 * math.pi * (n[:, None] * n[None, :] % FFT_HI) / FFT_HI
    cos, sin = np.cos(angle), np.sin(angle)
    last = np.block([[cos, -sin], [sin, cos]]) / math.sqrt(FFTLEN)
    return (*split_bf16(first), turns, *split_bf16(last))


def finish_kernel(
    data_ref, done, first_hi, first_lo, turns, last_hi, last_lo, out_hbm, out, done_sem, sem
):
    def place(src, half, pair, semaphore):
        return pltpu.make_async_copy(
            src.at[pair],
            out_hbm.at[:, pl.ds(2 * pair, 2), pl.ds(4 * half, 4), 0],
            semaphore,
        )

    for pair in range(PAIRS):
        place(done, 0, pair, done_sem).start()
    for pair in range(PAIRS):
        data = data_ref[pair].reshape(256, 256)
        store_pair(
            out, pair, transform_pair(data, first_hi, first_lo, turns, last_hi, last_lo)
        )
    for pair in range(PAIRS):
        place(out, 1, pair, sem).start()
    for pair in range(PAIRS):
        place(done, 0, pair, done_sem).wait()
    for pair in range(PAIRS):
        place(out, 1, pair, sem).wait()


def finish(second, spectra, tables):
    return pl.pallas_call(
        finish_kernel,
        out_shape=jax.ShapeDtypeStruct((2, 8, 8, 1, FFT_LO, FFT_HI), jnp.float32),
        in_specs=[pl.BlockSpec(memory_space=pltpu.VMEM)] * 7,
        out_specs=pl.BlockSpec(memory_space=pltpu.HBM),
        scratch_shapes=[
            pltpu.VMEM((PAIRS, 2, 2, 4, FFT_LO, FFT_HI), jnp.float32),
            pltpu.SemaphoreType.DMA,
            pltpu.SemaphoreType.DMA,
        ],
        compiler_params=pltpu.CompilerParams(vmem_limit_bytes=32 * 1024 * 1024),
    )(second, spectra, *tables)


def shards(strengths, sample_cell, sample_frac):
    tables = tuple(jnp.asarray(table) for table in transform_tables())
    second, spectra = spread(strengths, sample_cell, sample_frac, tables)
    return finish(second, spectra, tables)


def solution(mesh):
    placed = (P(None, "freq", None, "tm"), P("tm"), P("tm"))
    return jax.shard_map(
        shards,
        mesh=mesh,
        in_specs=placed,
        out_specs=P(None, None, "tm", "freq", None, None),
        check_vma=False,
    )
```

time: 41.3 us -> 39.3 us (0.952)
  the two profiles are of different devices: /device:TPU:11 before, /device:TPU:91 now
where the time goes in v3:
time: 39.3 us; the launch traced here: 39.2 us
  Pallas kernels  39.1 us (99%)
    pallas_call x1, Pallas kernels, spread(): pl.pallas_call(spread_kernel, out_shape=(jax.ShapeDtypeStruct(half_shape,...  37.2 us
    pallas_call x1, Pallas kernels, finish(): pl.pallas_call(finish_kernel, out_shape=jax.ShapeDtypeStruct((2, 8, 8, 1,...  1.93 us

profile of v3, /device:TPU:91, one launch (start us, length us, event | category | flops | bytes accessed | tf_op | source)
XLA Modules:
  0.0 39.2 jit_solution(1939314568483573902)
XLA Ops:
  0.0 0.0 copy-start
  0.0 0.0 copy-start.1
  0.0 0.0 copy-start.4
  0.0 0.0 copy-start.2
  0.0 0.0 copy-start.3
  0.0 37.2 %shard_map.82 = (bf16[4,4,2,4,8,256]{5,4,3,2,1,0:T(8,128)(2,1)S(1)}, f32[4,2,2,4,32,128]{5,4,3,2,1,0:T(8,128)S(1)}) custom-call(bf16[2,1,256,2048]{3,2,1,0:T(8,128)(2,1)} %strength_hbm.1, s32[1,2048]{1,0:T(1,128)} %bitcast.2, f32[1,2048]{1,0:T(1,128)} %bitcast.3, bf16[256,256]{1,0:T(8,128)(2,1)} %constant.10.clone.first_hi_hbm.first_hi, ...), custom_call_target="tpu_custom_call" | custom-call | tf_op jit(solution)/shard_map/pallas_call | solution.py:312
  37.2 0.0 copy-done
  37.2 0.0 copy-done.1
  37.2 0.0 copy-done.4
  37.2 0.0 copy-done.2
  37.2 0.0 copy-done.3
  37.2 1.9 %shard_map.83 = f32[2,8,8,1,32,128]{5,4,3,2,1,0:T(8,128)} custom-call(bf16[4,4,2,4,8,256]{5,4,3,2,1,0:T(8,128)(2,1)S(1)} %get-tuple-element.7.data_ref, f32[4,2,2,4,32,128]{5,4,3,2,1,0:T(8,128)S(1)} %get-tuple-element.8.done, bf16[256,256]{1,0:T(8,128)(2,1)S(1)} %copy-done.3, bf16[256,256]{1,0:T(8,128)(2,1)S(1)} %copy-done.2, f32[6,16,128]{2,1,0:T(8,128)S(1)} %copy-done.4, ...), custom_call_target="tpu_custom_call" | custom-call | tf_op jit(solution)/shard_map/pallas_call | solution.py:412
Async XLA Ops:
  0.0 37.2 %copy-start = (bf16[256,256]{1,0:T(8,128)(2,1)S(1)}, bf16[256,256]{1,0:T(8,128)(2,1)}, u32[]{:S(2)}) copy-start(bf16[256,256]{1,0:T(8,128)(2,1)} %constant.14.clone.last_lo_hbm.last_lo) | copy-start | bytes 393220
  0.0 37.2 %copy-start.1 = (bf16[256,256]{1,0:T(8,128)(2,1)S(1)}, bf16[256,256]{1,0:T(8,128)(2,1)}, u32[]{:S(2)}) copy-start(bf16[256,256]{1,0:T(8,128)(2,1)} %constant.13.clone.last_hi_hbm.last_hi) | copy-start | bytes 393220
  0.0 37.2 %copy-start.4 = (f32[6,16,128]{2,1,0:T(8,128)S(1)}, f32[6,16,128]{2,1,0:T(8,128)}, u32[]{:S(2)}) copy-start(f32[6,16,128]{2,1,0:T(8,128)} %constant.12.clone.turns_hbm.turns) | copy-start | bytes 147460
  0.0 37.2 %copy-start.2 = (bf16[256,256]{1,0:T(8,128)(2,1)S(1)}, bf16[256,256]{1,0:T(8,128)(2,1)}, u32[]{:S(2)}) copy-start(bf16[256,256]{1,0:T(8,128)(2,1)} %constant.11.clone.first_lo_hbm.first_lo) | copy-start | bytes 393220
  0.0 37.2 %copy-start.3 = (bf16[256,256]{1,0:T(8,128)(2,1)S(1)}, bf16[256,256]{1,0:T(8,128)(2,1)}, u32[]{:S(2)}) copy-start(bf16[256,256]{1,0:T(8,128)(2,1)} %constant.10.clone.first_hi_hbm.first_hi) | copy-start | bytes 393220

commit v4 on v3

--- a/solution.py
+++ b/solution.py
@@ -22,6 +22,8 @@
 CHUNK = GRID_DEV // CHUNKS
 TILE = 16
 HALVES = 2
+PIECES = 4
+PIECE = 512
 PAIRS = 4
 MESSAGE = (8, CHUNK)
 
@@ -77,6 +79,11 @@
     last_lo_hbm,
     second,
     spectra,
+    first_hi,
+    first_lo,
+    turns,
+    last_hi,
+    last_lo,
     cell_ref,
     frac_ref,
     strength,
@@ -86,11 +93,6 @@
     partial,
     halo,
     halo_in,
-    first_hi,
-    first_lo,
-    turns,
-    last_hi,
-    last_lo,
     load_sem,
     table_sem,
     send_sem,
@@ -106,7 +108,14 @@
     loads = [
         pltpu.make_async_copy(cell_hbm, cell_ref, load_sem.at[0]),
         pltpu.make_async_copy(frac_hbm, frac_ref, load_sem.at[1]),
-        pltpu.make_async_copy(strength_hbm, strength, load_sem.at[2]),
+        *(
+            pltpu.make_async_copy(
+                strength_hbm.at[:, :, :, pl.ds(piece * PIECE, PIECE)],
+                strength.at[:, :, :, pl.ds(piece * PIECE, PIECE)],
+                load_sem.at[2 + piece],
+            )
+            for piece in range(PIECES)
+        ),
     ]
     for load in loads:
         load.start()
@@ -135,9 +144,6 @@
             )
         )
     ]
-    for table in tables:
-        table.start()
-
     loads[0].wait()
     loads[1].wait()
     samples = cell_ref.shape[1]
@@ -226,13 +232,23 @@
         lax.fori_loop(0, 8, one, 0)
 
     build(1)
-    loads[2].wait()
-    round_out(1, gather(1))
-    build(2)
-    round_out(2, gather(2))
+    total = None
+    for piece in range(PIECES):
+        loads[2 + piece].wait()
+        span = slice(piece * PIECE, (piece + 1) * PIECE)
+        part = lax.dot_general(
+            strength[:, :, :, span].reshape(2 * strength.shape[2], PIECE),
+            window[CHUNK : 2 * CHUNK, span],
+            across,
+            preferred_element_type=jnp.float32,
+        )
+        total = part if total is None else total + part
+    round_out(1, total)
+    pl.semaphore_wait(barrier, 34)
+    send(0, 1, 1)
+    for table in tables:
+        table.start()
     halo[...] = lax.dot_general(edge_window, rows(), across, preferred_element_type=jnp.float32)
-
-    pl.semaphore_wait(barrier, 34)
     to_right = pltpu.make_async_remote_copy(
         src_ref=halo.at[0:8],
         dst_ref=halo_in.at[0:8],
@@ -251,8 +267,9 @@
     )
     to_right.start()
     to_left.start()
-    send(0, 1, 2)
-
+    build(2)
+    round_out(2, gather(2))
+    send(0, 2, 1)
     build(0)
     partial[0] = gather(0)
     build(3)
@@ -314,9 +331,10 @@
         out_shape=(
             jax.ShapeDtypeStruct(half_shape, jnp.bfloat16),
             jax.ShapeDtypeStruct((PAIRS, 2, 2, 4, FFT_LO, FFT_HI), jnp.float32),
+            *(jax.ShapeDtypeStruct(table.shape, table.dtype) for table in tables),
         ),
         in_specs=[pl.BlockSpec(memory_space=pltpu.HBM)] * len(inputs),
-        out_specs=(pl.BlockSpec(memory_space=pltpu.VMEM),) * 2,
+        out_specs=(pl.BlockSpec(memory_space=pltpu.VMEM),) * (2 + len(tables)),
         scratch_shapes=[
             pltpu.VMEM((1, samples), jnp.int32),
             pltpu.VMEM((1, samples), jnp.float32),
@@ -327,8 +345,7 @@
             pltpu.VMEM((2, rows, CHUNK), jnp.float32),
             pltpu.VMEM((16, rows), jnp.float32),
             pltpu.VMEM((128, rows), jnp.float32),
-            *(pltpu.VMEM(table.shape, table.dtype) for table in tables),
-            pltpu.SemaphoreType.DMA((3,)),
+            pltpu.SemaphoreType.DMA((2 + PIECES,)),
             pltpu.SemaphoreType.DMA((5,)),
             pltpu.SemaphoreType.DMA,
             pltpu.SemaphoreType.DMA((2,)),
@@ -425,7 +442,7 @@
 
 def shards(strengths, sample_cell, sample_frac):
     tables = tuple(jnp.asarray(table) for table in transform_tables())
-    second, spectra = spread(strengths, sample_cell, sample_frac, tables)
+    second, spectra, *tables = spread(strengths, sample_cell, sample_frac, tables)
     return finish(second, spectra, tables)
 
 

time: 39.3 us -> 39 us (level)
  the two profiles are of different devices: /device:TPU:91 before, /device:TPU:3 now
where the time goes in v4:
time: 39 us; the launch traced here: 38.9 us
  Pallas kernels  38.9 us (100%)
    pallas_call x1, Pallas kernels, spread(): pl.pallas_call(spread_kernel, out_shape=(jax.ShapeDtypeStruct(half_shape,...  37 us
    pallas_call x1, Pallas kernels, finish(): pl.pallas_call(finish_kernel, out_shape=jax.ShapeDtypeStruct((2, 8, 8, 1,...  1.93 us

profile of v4, /device:TPU:3, one launch (start us, length us, event | category | flops | bytes accessed | tf_op | source)
XLA Modules:
  0.0 38.9 jit_solution(7416193494982798233)
XLA Ops:
  0.0 37.0 %shard_map.82 = (bf16[4,4,2,4,8,256]{5,4,3,2,1,0:T(8,128)(2,1)S(1)}, f32[4,2,2,4,32,128]{5,4,3,2,1,0:T(8,128)S(1)}, bf16[256,256]{1,0:T(8,128)(2,1)S(1)}, bf16[2...) custom-call(bf16[2,1,256,2048]{3,2,1,0:T(8,128)(2,1)} %strength_hbm., ...), custom_call_target="tpu_custom_call" | custom-call | tf_op jit(solution)/shard_map/pallas_call | solution.py:329
  37.0 1.9 %shard_map.83 = f32[2,8,8,1,32,128]{5,4,3,2,1,0:T(8,128)} custom-call(bf16[4,4,2,4,8,256]{5,4,3,2,1,0:T(8,128)(2,1)S(1)} %get-tuple-element.12.data_ref, f32[4,2,2,4,32,128]{5,4,3,2,1,0:T(8,128)S(1)} %get-tuple-element.13.done, bf16[256,256]{1,0:T(8,128)(2,1)S(1)} %get-tuple-element.14.first_hi, bf16[256,256]{1,0:T(8,128)(2,1)S(1)} %get-tuple-element.15.first_lo, ...), custom_call_target="tpu_custom_call" | custom-call | tf_op jit(solution)/shard_map/pallas_call | solution.py:429

commit v5 on v4

--- a/solution.py
+++ b/solution.py
@@ -28,8 +28,9 @@
 MESSAGE = (8, CHUNK)
 
 
-def plane(step, own):
-    shift = ((step + 1) >> 1) * (2 * (step & 1) - 1)
+def plane(step, own, far):
+    count = (1 - far) * step + far * (7 - step)
+    shift = ((count + 1) >> 1) * (2 * (count & 1) - 1)
     return (own + shift + 8) & 7
 
 
@@ -197,12 +198,12 @@
         (((block >> 4) + (inner >> 1)) & 1) * 16 + ((block + inner) & 1) for inner in range(4)
     ]
 
-    def send(half, begin, count):
+    def send(half, begin, count, far=0):
         landing = (first, second)[half]
         dst = landing.at[group // 2, block % 4, group % 2, pl.ds(begin, count)]
 
         def one(step, carry):
-            position = plane(step, own_plane)
+            position = plane(step, own_plane, far)
             for inner in range(4):
                 target = offsets[inner] + 2 * position
                 src = outgoing.at[half, target, pl.ds(begin, count)]
@@ -283,11 +284,11 @@
     round_out(
         0, partial[0] + jnp.concatenate([jnp.where(lane < 8, beyond, 0.0), none], axis=1)
     )
-    send(0, 0, 1)
+    send(0, 0, 1, 1)
     round_out(
         3, partial[1] + jnp.concatenate([none, jnp.where(lane >= 120, beyond, 0.0)], axis=1)
     )
-    send(0, 3, 1)
+    send(0, 3, 1, 1)
     send(1, 0, 4)
 
     for table in tables:
@@ -401,28 +402,32 @@
 
 
 def finish_kernel(
-    data_ref, done, first_hi, first_lo, turns, last_hi, last_lo, out_hbm, out, done_sem, sem
+    data_ref, done, first_hi, first_lo, turns, last_hi, last_lo, out_hbm, *scratch
 ):
+    *outs, done_sem, sem = scratch
+
     def place(src, half, pair, semaphore):
         return pltpu.make_async_copy(
-            src.at[pair],
-            out_hbm.at[:, pl.ds(2 * pair, 2), pl.ds(4 * half, 4), 0],
-            semaphore,
-        )
-
+            src, out_hbm.at[:, pl.ds(2 * pair, 2), pl.ds(4 * half, 4), 0], semaphore
+        )
+
+    early = [place(done.at[pair], 0, pair, done_sem) for pair in range(PAIRS)]
+    late = [place(outs[pair].at[0], 1, pair, sem) for pair in range(PAIRS)]
+    for copy in early:
+        copy.start()
+    results = [
+        transform_pair(
+            data_ref[pair].reshape(256, 256), first_hi, first_lo, turns, last_hi, last_lo
+        )
+        for pair in range(PAIRS)
+    ]
     for pair in range(PAIRS):
-        place(done, 0, pair, done_sem).start()
-    for pair in range(PAIRS):
-        data = data_ref[pair].reshape(256, 256)
-        store_pair(
-            out, pair, transform_pair(data, first_hi, first_lo, turns, last_hi, last_lo)
-        )
-    for pair in range(PAIRS):
-        place(out, 1, pair, sem).start()
-    for pair in range(PAIRS):
-        place(done, 0, pair, done_sem).wait()
-    for pair in range(PAIRS):
-        place(out, 1, pair, sem).wait()
+        store_pair(outs[pair], 0, results[pair])
+        if pair > 0:
+            late[pair - 1].start()
+    late[PAIRS - 1].start()
+    for copy in early + late:
+        copy.wait()
 
 
 def finish(second, spectra, tables):
@@ -432,7 +437,7 @@
         in_specs=[pl.BlockSpec(memory_space=pltpu.VMEM)] * 7,
         out_specs=pl.BlockSpec(memory_space=pltpu.HBM),
         scratch_shapes=[
-            pltpu.VMEM((PAIRS, 2, 2, 4, FFT_LO, FFT_HI), jnp.float32),
+            *(pltpu.VMEM((1, 2, 2, 4, FFT_LO, FFT_HI), jnp.float32),) * PAIRS,
             pltpu.SemaphoreType.DMA,
             pltpu.SemaphoreType.DMA,
         ],

time: 39 us -> 38.9 us (level)
  the two profiles are of different devices: /device:TPU:3 before, /device:TPU:19 now
where the time goes in v5:
time: 38.9 us; the launch traced here: 38.8 us
  Pallas kernels  38.8 us (100%)
    pallas_call x1, Pallas kernels, spread(): pl.pallas_call(spread_kernel, out_shape=(jax.ShapeDtypeStruct(half_shape,...  37 us
    pallas_call x1, Pallas kernels, finish(): pl.pallas_call(finish_kernel, out_shape=jax.ShapeDtypeStruct((2, 8, 8, 1,...  1.77 us

profile of v5, /device:TPU:19, one launch (start us, length us, event | category | flops | bytes accessed | tf_op | source)
XLA Modules:
  0.0 38.8 jit_solution(9710355854719942150)
XLA Ops:
  0.0 37.0 %shard_map.82 = (bf16[4,4,2,4,8,256]{5,4,3,2,1,0:T(8,128)(2,1)S(1)}, f32[4,2,2,4,32,128]{5,4,3,2,1,0:T(8,128)S(1)}, bf16[256,256]{1,0:T(8,128)(2,1)S(1)}, bf16[2...) custom-call(bf16[2,1,256,2048]{3,2,1,0:T(8,128)(2,1)} %strength_hbm., ...), custom_call_target="tpu_custom_call" | custom-call | tf_op jit(solution)/shard_map/pallas_call | solution.py:330
  37.0 1.8 %shard_map.83 = f32[2,8,8,1,32,128]{5,4,3,2,1,0:T(8,128)} custom-call(bf16[4,4,2,4,8,256]{5,4,3,2,1,0:T(8,128)(2,1)S(1)} %get-tuple-element.12.data_ref, f32[4,2,2,4,32,128]{5,4,3,2,1,0:T(8,128)S(1)} %get-tuple-element.13.done, bf16[256,256]{1,0:T(8,128)(2,1)S(1)} %get-tuple-element.14.first_hi, bf16[256,256]{1,0:T(8,128)(2,1)S(1)} %get-tuple-element.15.first_lo, ...), custom_call_target="tpu_custom_call" | custom-call | tf_op jit(solution)/shard_map/pallas_call | solution.py:434
